TPU v7x, 256 devices: a whole 4x4x8 slice. The times are simulated.
256 devices in a mesh: mp: 64 (over z, x, core), head: 4 (over y).
Axes of the slice: x: 4, y: 4, z: 8, core: 2. Of those that a mesh axis runs over, the one named last changes fastest.
Arguments:
- hidden: bfloat16 [8, 4096], replicated, may hold values from -6 to 6
- norm_gain: float32 [4096], replicated, may hold values from 0.25 to 1.75
- w_query: bfloat16 [4096, 4096], P('mp', 'head'), may hold values from -0.09375 to 0.09375
- enc_states: bfloat16 [8, 4096, 4096], P(None, 'mp'), may hold values from -6 to 6
- w_key: bfloat16 [4096, 4096], P('mp', 'head'), may hold values from -0.09375 to 0.09375
- w_value: bfloat16 [4096, 4096], P('mp', 'head'), may hold values from -0.09375 to 0.09375
- w_out: bfloat16 [4096, 4096], P('head', 'mp'), may hold values from -0.09375 to 0.09375
- bias_table: float32 [32, 64], P(None, 'head'), may hold values from -5 to 300
- buckets: int32 [8, 4096], P(None, 'mp'), may hold values from 0 to 31
- src_len: int32 [8], replicated, may hold values from 512 to 4096
Outputs:
- updated: bfloat16 [8, 4096], P(None, 'mp')
All inputs are finite; a program needn't handle non-finite values.
Results may differ from a plain program's by a relative error of at most 0.0049.
Values may be sent and summed in bfloat16 or wider, within the bound.
A program may use at most 128 MiB of HBM per device.

v0:
```python
import jax
import jax.numpy as jnp
from jax import lax
from jax.sharding import PartitionSpec as P

EPSILON = 1e-06
NEGATIVE = -1e30


def shards(
    hidden, norm_gain, w_query, enc_states, w_key, w_value, w_out, bias_table, buckets, src_len
):
    batch, src_local, _ = enc_states.shape
    rows, inner = w_key.shape
    heads = bias_table.shape[1]
    head_size = inner // heads
    me = lax.axis_index("mp")
    widened = hidden.astype(jnp.float32)
    mean_square = jnp.mean(widened * widened, axis=-1, keepdims=True)
    normed = (widened * lax.rsqrt(mean_square + EPSILON) * norm_gain).astype(jnp.bfloat16)
    mine = lax.dynamic_slice_in_dim(normed, me * rows, rows, 1)
    query = jnp.dot(mine, w_query, preferred_element_type=jnp.float32)
    query = lax.psum(query, "mp").astype(jnp.bfloat16).reshape(batch, heads, head_size)
    probe = jnp.einsum(
        "bhe,dhe->bhd",
        query,
        w_key.reshape(rows, heads, head_size),
        preferred_element_type=jnp.float32,
    )
    probe = (probe * float(head_size) ** (-0.5)).astype(jnp.bfloat16)
    probe = lax.all_gather(probe, "mp", axis=2, tiled=True)
    scores = jnp.einsum("bhd,bsd->bhs", probe, enc_states, preferred_element_type=jnp.float32)
    ids = jnp.arange(bias_table.shape[0], dtype=jnp.int32)
    one_hot = (buckets[:, :, None] == ids[None, None, :]).astype(jnp.float32)
    scores = scores + jnp.einsum(
        "bsk,kh->bhs", one_hot, bias_table, precision=lax.Precision.HIGHEST
    )
    positions = me * src_local + jnp.arange(src_local, dtype=jnp.int32)
    live = (positions[None, :] < src_len[:, None])[:, None, :]
    scores = jnp.where(live, scores, NEGATIVE)
    top = lax.pmax(jnp.max(scores, axis=-1), "mp")
    weights = jnp.where(live, jnp.exp(scores - top[:, :, None]), 0.0)
    total = lax.psum(jnp.sum(weights, axis=-1), "mp")
    mixed = jnp.einsum(
        "bhs,bsd->bhd", weights.astype(jnp.bfloat16), enc_states, preferred_element_type=jnp.float32
    )
    mixed = lax.psum_scatter(mixed, "mp", scatter_dimension=2, tiled=True)
    mixed = (mixed / total[:, :, None]).astype(jnp.bfloat16)
    context = jnp.einsum(
        "bhd,dhe->bhe",
        mixed,
        w_value.reshape(rows, heads, head_size),
        preferred_element_type=jnp.float32,
    )
    context = lax.psum(context, "mp").astype(jnp.bfloat16).reshape(batch, inner)
    out = lax.psum(jnp.dot(context, w_out, preferred_element_type=jnp.float32), "head")
    cols = w_out.shape[1]
    residual = lax.dynamic_slice_in_dim(widened, me * cols, cols, 1)
    return (out + residual).astype(jnp.bfloat16)


def solution(mesh):
    in_specs = (
        P(),
        P(),
        P("mp", "head"),
        P(None, "mp", None),
        P("mp", "head"),
        P("mp", "head"),
        P("head", "mp"),
        P(None, "head"),
        P(None, "mp"),
        P(),
    )
    return jax.shard_map(
        shards, mesh=mesh, in_specs=in_specs, out_specs=P(None, "mp"), check_vma=False
    )
```

profile of v0, /device:TPU:0, one launch (start us, length us, event | category | flops | bytes accessed | tf_op | source)
XLA Modules:
  0.0 922.8 jit_solution(14839864621208806205)
XLA Ops:
  6.5 0.9 convert_element_type.28
  7.4 1.0 multiply_reduce_fusion
  8.4 0.8 dynamic-slice
  9.2 0.2 fusion.19
  9.4 251.9 %psum.28 = bf16[8,1024]{1,0:T(8,128)(2,1)S(1)} all-reduce(f32[8,1024]{1,0:T(8,128)S(1)} %fusion.19), channel_id=1, replica_groups=mesh['mp'=64,'head'=4] {'mp'}, use_global_device_ids=true, to_apply=%region_1.0 | all-reduce | flops 8192 | bytes 49152 | tf_op jit(solution)/shard_map/psum | solution.py:23
  261.4 1.1 reshape.52
  262.5 0.3 fusion.5
  262.7 0.8 copy.16
  263.6 0.7 broadcast_compare_fusion
  264.4 77.1 %all-gather.2.cloned.1.call-done = bf16[8,16,4096]{1,0,2:T(8,128)(2,1)} async-done(((bf16[8,16,64]{1,0,2:T(8,128)(2,1)}), bf16[8,16,4096]{1,0,2:T(8,128)(2,1)}) %all-gather.2.cloned.1.call-update) | async-done | bytes 1048592 | tf_op jit(solution)/shard_map/all_gather | solution.py:31
  341.5 7.3 fusion
  348.8 0.3 fusion.24
  349.1 126.0 %pmax.7 = f32[8,16]{1,0:T(8,128)S(1)} all-reduce(f32[8,16]{1,0:T(8,128)S(1)} %get-tuple-element.5), channel_id=1, replica_groups=mesh['mp'=64,'head'=4] {'mp'}, use_global_device_ids=true, to_apply=%region_3.4 | all-reduce | flops 128 | bytes 1024 | tf_op jit(solution)/shard_map/pmax | solution.py:41
  475.1 2.9 fusion.11
  478.0 16.8 %copy.22 = f32[8,16,4096]{0,1,2:T(8,128)} copy(f32[8,16,4096]{2,1,0:T(8,128)S(1)} %fusion.11) | data formatting | bytes 4194304
  494.8 23.7 %reshape.56 = f32[4096,128]{1,0:T(8,128)} reshape(f32[4096,16,8]{2,1,0:T(8,128)} %bitcast.23) | data formatting | bytes 4194304
  518.9 124.3 %psum.29 = f32[8,16]{1,0:T(8,128)S(1)} all-reduce(f32[8,16]{1,0:T(8,128)S(1)} %fusion.9), channel_id=1, replica_groups=mesh['mp'=64,'head'=4] {'mp'}, use_global_device_ids=true, to_apply=%region_6.7 | all-reduce | flops 128 | bytes 1024 | tf_op jit(solution)/shard_map/psum | solution.py:43
  643.3 13.6 %reduce-scatter.4.cloned.1.call-done = f32[64,128]{1,0:T(8,128)} async-done(((f32[4096,128]{1,0:T(8,128)}), f32[64,128]{1,0:T(8,128)}) %reduce-scatter.4.cloned.1.call-update) | async-done | bytes 32784
  656.9 1.0 reshape.57
  658.0 0.2 copy.23
  658.2 0.2 convolution_bitcast_fusion
  658.5 246.1 %psum.30 = bf16[8,16,64]{2,0,1:T(8,128)(2,1)S(1)} all-reduce(f32[8,16,64]{2,0,1:T(8,128)S(1)} %convolution_bitcast_fusion), channel_id=1, replica_groups=mesh['mp'=64,'head'=4] {'mp'}, use_global_device_ids=true, to_apply=%region_7.8 | all-reduce | flops 8192 | bytes 49152 | tf_op jit(solution)/shard_map/psum | solution.py:55
  904.9 10.5 %psum.31 = f32[8,64]{1,0:T(8,128)S(1)} all-reduce(f32[8,64]{1,0:T(8,128)S(1)} %fusion.25), channel_id=1, replica_groups=mesh['mp'=64,'head'=4] {'head'}, use_global_device_ids=true, to_apply=%region_8.9 | all-reduce | flops 512 | bytes 4096 | tf_op jit(solution)/shard_map/psum | solution.py:56
  915.3 0.7 add_convert_fusion
  (23 shorter events, 0.9 us)
Async XLA Ops:
  6.5 2.7 copy-start
  6.5 334.9 %all-gather.2.cloned.1.call-start = ((), (), s32[]{:S(2)}) async-start(), calls=%async_computation.1 | async-start | bytes 8519680 | tf_op jit(solution)/shard_map/all_gather | solution.py:31
  263.6 393.4 %reduce-scatter.4.cloned.1.call-start = ((), (), s32[]{:S(2)}) async-start(), calls=%async_computation.2 | async-start | bytes 2129920
  264.4 84.4 %copy-start.3 = (f32[32,16]{0,1:T(8,128)S(1)}, f32[32,16]{0,1:T(8,128)}, u32[]{:S(2)}) copy-start(f32[32,16]{0,1:T(8,128)} %param.17) | copy-start | bytes 6148
  264.4 84.4 %copy-start.4 = (s32[8,64]{1,0:T(8,128)S(1)}, s32[8,64]{1,0:T(8,128)}, u32[]{:S(2)}) copy-start(s32[8,64]{1,0:T(8,128)} %param.18) | copy-start | bytes 6148
  494.8 23.7 %copy-start.1 = (bf16[64,1024]{1,0:T(8,128)(2,1)S(1)}, bf16[64,1024]{1,0:T(8,128)(2,1)}, u32[]{:S(2)}) copy-start(bf16[64,1024]{1,0:T(8,128)(2,1)} %param.15) | copy-start | bytes 393220
  518.5 386.2 %copy-start.2 = (bf16[1024,64]{0,1:T(8,128)(2,1)S(1)}, bf16[1024,64]{0,1:T(8,128)(2,1)}, u32[]{:S(2)}) copy-start(bf16[1024,64]{0,1:T(8,128)(2,1)} %param.16) | copy-start | bytes 393220
Sparse Core Ops, SparseCore 0:
  263.7 77.7 all-gather.1
  518.7 138.2 reduce-scatter.3
where the time goes:
time: 924 us; the launch traced here: 923 us
  blocking collectives  759 us (82%)
  waiting for transfers between devices  90.8 us (10%)
  local copies, waits for them, and re-layouts  45 us (5%)
  between operations  13.5 us (1%)
  matrix products  11.3 us (1%)
    psum x1, blocking collectives, shards(): lax.psum(query, 'mp').astype(jnp.bfloat16).reshape(batch, heads, head_size)  252 us
    psum x1, blocking collectives, shards(): context = lax.psum(context, 'mp').astype(jnp.bfloat16).reshape(batch, inner)  246 us
    pmax x1, blocking collectives, shards(): top = lax.pmax(jnp.max(scores, axis=-1), 'mp')  126 us
    psum x1, blocking collectives, shards(): total = lax.psum(jnp.sum(weights, axis=-1), 'mp')  124 us
    all_gather x1, waiting for transfers between devices, shards(): probe = lax.all_gather(probe, 'mp', axis=2, tiled=True)  77.1 us
    unnamed x14, local copies, waits for them, and re-layouts  41.8 us
  transfers between devices with their start and end apart: 2, of which 2 were waited for; matrix products, arithmetic and copies ran while one was open for 0% of the time, Pallas kernels for 0%

commit v1 on v0

--- a/solution.py
+++ b/solution.py
@@ -28,7 +28,10 @@
         preferred_element_type=jnp.float32,
     )
     probe = (probe * float(head_size) ** (-0.5)).astype(jnp.bfloat16)
-    probe = lax.all_gather(probe, "mp", axis=2, tiled=True)
+    n_dev = lax.axis_size("mp")
+    shards_2 = jnp.stack([probe for _ in range(n_dev)])
+    shards_2 = lax.all_to_all(shards_2, "mp", split_axis=0, concat_axis=0)
+    probe = jnp.concatenate(shards_2, axis=2)
     scores = jnp.einsum("bhd,bsd->bhs", probe, enc_states, preferred_element_type=jnp.float32)
     ids = jnp.arange(bias_table.shape[0], dtype=jnp.int32)
     one_hot = (buckets[:, :, None] == ids[None, None, :]).astype(jnp.float32)

time: 924 us -> 884 us (0.957)
  waiting for transfers between devices: 90.8 us -> 42.8 us
  local copies, waits for them, and re-layouts: 45 us -> 54.4 us
    all_gather x1 -> x0, waiting for transfers between devices: 77.1 us -> none  [shards(): probe = lax.all_gather(probe, 'mp', axis=2, tiled=True)]
    all_to_all x0 -> x1, waiting for transfers between devices: none -> 28.7 us  [shards(): shards_2 = lax.all_to_all(shards_2, 'mp', split_axis=0, concat_axis=0)]
    unnamed x14 -> x18, local copies, waits for them, and re-layouts: 41.8 us -> 45.5 us
where the time goes in v1:
time: 884 us; the launch traced here: 883 us
  blocking collectives  758 us (86%)
  local copies, waits for them, and re-layouts  54.4 us (6%)
  waiting for transfers between devices  42.8 us (5%)
  between operations  13.5 us (2%)
    psum x1, blocking collectives, shards(): lax.psum(query, 'mp').astype(jnp.bfloat16).reshape(batch, heads, head_size)  252 us
    psum x1, blocking collectives, shards(): context = lax.psum(context, 'mp').astype(jnp.bfloat16).reshape(batch, inner)  246 us
    pmax x1, blocking collectives, shards(): top = lax.pmax(jnp.max(scores, axis=-1), 'mp')  125 us
    psum x1, blocking collectives, shards(): total = lax.psum(jnp.sum(weights, axis=-1), 'mp')  124 us
    unnamed x18, local copies, waits for them, and re-layouts  45.5 us
    all_to_all x1, waiting for transfers between devices, shards(): shards_2 = lax.all_to_all(shards_2, 'mp', split_axis=0, concat_axis=0)  28.7 us
  transfers between devices with their start and end apart: 2, of which 2 were waited for; matrix products, arithmetic and copies ran while one was open for 0% of the time, Pallas kernels for 0%

profile of v1, /device:TPU:0, one launch (start us, length us, event | category | flops | bytes accessed | tf_op | source)
XLA Modules:
  0.0 883.5 jit_solution(15381726098975800439)
XLA Ops:
  6.5 0.9 convert_element_type.28
  7.4 1.0 multiply_reduce_fusion
  8.4 0.8 dynamic-slice
  9.4 251.9 %psum.28 = bf16[8,1024]{1,0:T(8,128)(2,1)S(1)} all-reduce(f32[8,1024]{1,0:T(8,128)S(1)} %fusion.17), channel_id=1, replica_groups=mesh['mp'=64,'head'=4] {'mp'}, use_global_device_ids=true, to_apply=%region_1.0 | all-reduce | flops 8192 | bytes 49152 | tf_op jit(solution)/shard_map/psum | solution.py:23
  261.4 1.1 reshape.60
  262.7 0.5 stack.2
  263.3 2.3 reshape.68
  265.6 4.7 all-to-all-start
  270.4 28.7 %all-to-all-done = bf16[64,2,4096]{2,1,0:T(2,128)(2,1)S(1)} async-done(((bf16[64,2,4096]{2,1,0:T(2,128)(2,1)}), bf16[64,2,4096]{2,1,0:T(2,128)(2,1)S(1)}, u32[]{:S(2)}, u32[]{:S(2)}) %all-to-all-start) | async-done | bytes 1048608 | tf_op jit(solution)/shard_map/all_to_all | solution.py:33
  299.1 1.3 reshape.69
  300.4 2.7 copy.23
  303.2 3.3 reshape.62
  306.5 3.4 fusion.23
  309.9 0.3 fusion.22
  310.2 125.2 %pmax.7 = f32[8,16]{1,0:T(8,128)S(1)} all-reduce(f32[8,16]{1,0:T(8,128)S(1)} %get-tuple-element.5), channel_id=1, replica_groups=mesh['mp'=64,'head'=4] {'mp'}, use_global_device_ids=true, to_apply=%region_3.4 | all-reduce | flops 128 | bytes 1024 | tf_op jit(solution)/shard_map/pmax | solution.py:44
  435.4 2.9 fusion.9
  438.3 16.8 %copy.28 = f32[8,16,4096]{0,1,2:T(8,128)} copy(f32[8,16,4096]{2,1,0:T(8,128)S(1)} %fusion.9) | data formatting | bytes 4194304
  455.1 23.7 %reshape.66 = f32[4096,128]{1,0:T(8,128)} reshape(f32[4096,16,8]{2,1,0:T(8,128)} %bitcast.27) | data formatting | bytes 4194304
  479.2 124.2 %psum.29 = f32[8,16]{1,0:T(8,128)S(1)} all-reduce(f32[8,16]{1,0:T(8,128)S(1)} %fusion.7), channel_id=1, replica_groups=mesh['mp'=64,'head'=4] {'mp'}, use_global_device_ids=true, to_apply=%region_6.7 | all-reduce | flops 128 | bytes 1024 | tf_op jit(solution)/shard_map/psum | solution.py:46
  603.5 14.1 %reduce-scatter.4.cloned.1.call-done = f32[64,128]{1,0:T(8,128)} async-done(((f32[4096,128]{1,0:T(8,128)}), f32[64,128]{1,0:T(8,128)}) %reduce-scatter.4.cloned.1.call-update) | async-done | bytes 32784
  617.6 1.0 reshape.67
  619.1 246.1 %psum.30 = bf16[8,16,64]{2,0,1:T(8,128)(2,1)S(1)} all-reduce(f32[8,16,64]{2,0,1:T(8,128)S(1)} %convolution_bitcast_fusion), channel_id=1, replica_groups=mesh['mp'=64,'head'=4] {'mp'}, use_global_device_ids=true, to_apply=%region_7.8 | all-reduce | flops 8192 | bytes 49152 | tf_op jit(solution)/shard_map/psum | solution.py:58
  865.5 10.5 %psum.31 = f32[8,64]{1,0:T(8,128)S(1)} all-reduce(f32[8,64]{1,0:T(8,128)S(1)} %fusion.24), channel_id=1, replica_groups=mesh['mp'=64,'head'=4] {'head'}, use_global_device_ids=true, to_apply=%region_8.9 | all-reduce | flops 512 | bytes 4096 | tf_op jit(solution)/shard_map/psum | solution.py:59
  876.0 0.7 add_convert_fusion
  (29 shorter events, 1.9 us)
Async XLA Ops:
  6.5 2.7 copy-start
  9.2 261.1 %copy-start.5 = (s32[8]{0:T(128)S(1)}, s32[8]{0:T(128)}, u32[]{:S(2)}) copy-start(s32[8]{0:T(128)} %param.19) | copy-start | bytes 100
  265.6 33.5 %all-to-all-start = ((bf16[64,2,4096]{2,1,0:T(2,128)(2,1)}), bf16[64,2,4096]{2,1,0:T(2,128)(2,1)S(1)}, u32[]{:S(2)}, u32[]{:S(2)}) async-start(bf16[64,2,4096]{2,1,0:T(2,128)(2,1)} %reshape.68), calls=%async_computation | async-start | bytes 2097152 | tf_op jit(solution)/shard_map/all_to_all | solution.py:33
  270.2 347.3 %reduce-scatter.4.cloned.1.call-start = ((), (), s32[]{:S(2)}) async-start(), calls=%async_computation.2 | async-start | bytes 2129920
  303.2 6.7 copy-start.3
  303.2 6.7 copy-start.4
  455.1 23.7 %copy-start.1 = (bf16[64,1024]{1,0:T(8,128)(2,1)S(1)}, bf16[64,1024]{1,0:T(8,128)(2,1)}, u32[]{:S(2)}) copy-start(bf16[64,1024]{1,0:T(8,128)(2,1)} %param.15) | copy-start | bytes 393220
  478.8 386.6 %copy-start.2 = (bf16[1024,64]{0,1:T(8,128)(2,1)S(1)}, bf16[1024,64]{0,1:T(8,128)(2,1)}, u32[]{:S(2)}) copy-start(bf16[1024,64]{0,1:T(8,128)(2,1)} %param.16) | copy-start | bytes 393220
Sparse Core Ops, SparseCore 0:
  479.0 138.5 reduce-scatter.3
